TPU v7x, 32 devices: a whole 2x2x4 slice. The times are simulated.
32 devices in a mesh: seq: 8 (over z, y), tensor: 4 (over x, core).
Axes of the slice: x: 2, y: 2, z: 4, core: 2. Of those that a mesh axis runs over, the one named last changes fastest.
Arguments:
- layer_input: bfloat16 [2048, 4096], P('seq', 'tensor'), may hold values from -6 to 6
- norm_gain: float32 [4096], replicated, may hold values from 0.1 to 1.9
- in_weights: bfloat16 [2, 4096, 2048], P(None, None, 'tensor'), may hold values from -0.09375 to 0.09375
- conv_weight: float32 [4, 2048], P(None, 'tensor'), may hold values from -4 to 4
- conv_bias: float32 [2048], P('tensor'), may hold values from -3 to 3
- gate_weights: bfloat16 [2, 8, 256, 256], P(None, 'tensor'), may hold values from -0.375 to 0.375
- gate_bias: float32 [2, 2048], P(None, 'tensor'), may hold values from -4 to 4
- decay_rate: float32 [2048], P('tensor'), may hold values from 1e-06 to 0.03, as said below
- out_weight: bfloat16 [2048, 4096], P('tensor'), may hold values from -0.1875 to 0.1875
- mlp_gain: float32 [4096], replicated, may hold values from 0.1 to 1.9
- mlp_in: bfloat16 [2, 4096, 6144], P(None, 'seq', 'tensor'), may hold values from -0.09375 to 0.09375
- mlp_out: bfloat16 [6144, 4096], P('tensor', 'seq'), may hold values from -0.109375 to 0.109375
Outputs:
- block_output: bfloat16 [2048, 4096], P('seq', 'tensor')
Inputs may be any that keep to these rules, and one draw needn't show every extreme that they name: `decay_rate`: every rate is positive.
All inputs are finite; a program needn't handle non-finite values.
Results may differ from a plain program's by a relative error of at most 0.015.
Values may be sent and summed in bfloat16 or wider, within the bound.
A program may use at most 128 MiB of HBM per device.

v0:
```python
import jax
import jax.numpy as jnp
from jax import lax
from jax.sharding import PartitionSpec as P


def shifted(value, axis, steps):
    count = lax.axis_size(axis)
    first, last = (max(0, -steps), min(count, count - steps))
    return lax.ppermute(value, axis, [(source, source + steps) for source in range(first, last)])


def prefix(value, axis, combine, identity):
    size, here = (lax.axis_size(axis), lax.axis_index(axis))
    everything = jax.tree.map(lambda part: lax.all_gather(part, axis), value)
    start = jax.tree.map(
        lambda part, zero: jnp.broadcast_to(jnp.asarray(zero, part.dtype), part.shape),
        value,
        identity,
    )

    def hop(k, before):
        reached = k < here
        new = combine(before, jax.tree.map(lambda part: part[k], everything))
        return jax.tree.map(lambda a, b: jnp.where(reached, a, b), new, before)

    return lax.fori_loop(0, size, hop, start)


def rms_scale(rows, gain):
    values = rows.astype(jnp.float32)
    mean_square = jnp.mean(values * values, axis=-1, keepdims=True)
    return (values * lax.rsqrt(mean_square + 1e-06) * gain).astype(jnp.bfloat16)


def chain_step(earlier, later):
    return (earlier[0] * later[0], later[0] * earlier[1] + later[1])


def shards(
    layer_input,
    norm_gain,
    in_weights,
    conv_weight,
    conv_bias,
    gate_weights,
    gate_bias,
    decay_rate,
    out_weight,
    mlp_gain,
    mlp_in,
    mlp_out,
):
    whole_rows = lax.all_gather(layer_input, "tensor", axis=1, tiled=True)
    normed = rms_scale(whole_rows, norm_gain)
    branch_x = jnp.dot(normed, in_weights[0], preferred_element_type=jnp.float32).astype(
        jnp.bfloat16
    )
    branch_y = jax.nn.gelu(
        jnp.dot(normed, in_weights[1], preferred_element_type=jnp.float32), approximate=True
    )
    num_tokens = branch_x.shape[0]
    rim_rows = conv_weight.shape[0] - 1
    earlier_rows = shifted(branch_x[num_tokens - rim_rows :], "seq", 1)
    padded = jnp.concatenate([earlier_rows, branch_x], axis=0).astype(jnp.float32)
    convolved = jnp.zeros(branch_x.shape, jnp.float32) + conv_bias
    for tap_index in range(conv_weight.shape[0]):
        start_row = rim_rows - tap_index
        convolved = convolved + conv_weight[tap_index] * padded[start_row : start_row + num_tokens]
    conv_out = convolved.astype(jnp.bfloat16)
    local_blocks = gate_weights.shape[1]
    block_width = gate_weights.shape[2]
    blocks_in = conv_out.reshape(num_tokens, local_blocks, block_width)
    gate_pre = jnp.einsum(
        "tnc,knce->ktne", blocks_in, gate_weights, preferred_element_type=jnp.float32
    )
    gate_pre = gate_pre.reshape(2, num_tokens, local_blocks * block_width) + gate_bias[:, None, :]
    log_decay = -8.0 * jax.nn.sigmoid(gate_pre[0]) * decay_rate
    decay = jnp.exp(log_decay)
    driven = (
        conv_out.astype(jnp.float32)
        * jax.nn.sigmoid(gate_pre[1])
        * jnp.sqrt(-jnp.expm1(2.0 * log_decay))
    )
    cum_decay, cum_state = lax.associative_scan(chain_step, (decay, driven), axis=0)
    identity = (jnp.ones_like(cum_decay[-1]), jnp.zeros_like(cum_state[-1]))
    entering = prefix((cum_decay[-1], cum_state[-1]), "seq", chain_step, identity)
    carried = entering[1]
    state = cum_decay * carried + cum_state
    mixed = (state * branch_y).astype(jnp.bfloat16)
    partial_sums = jnp.dot(mixed, out_weight, preferred_element_type=jnp.float32)
    full_sums = lax.psum(partial_sums.astype(jnp.bfloat16), "tensor").astype(jnp.float32)
    mid_full = (whole_rows.astype(jnp.float32) + full_sums).astype(jnp.bfloat16)
    own_width = layer_input.shape[1]
    residual = lax.dynamic_slice_in_dim(
        mid_full, lax.axis_index("tensor") * own_width, own_width, 1
    )
    mlp_normed = rms_scale(mid_full, mlp_gain)
    gate_up = jnp.einsum(
        "tr,krf->ktf",
        mlp_normed,
        lax.all_gather(mlp_in, "seq", axis=1, tiled=True),
        preferred_element_type=jnp.float32,
    )
    hidden = (jax.nn.gelu(gate_up[0], approximate=True) * gate_up[1]).astype(jnp.bfloat16)
    down_terms = jnp.dot(
        hidden,
        lax.all_gather(mlp_out, "seq", axis=1, tiled=True),
        preferred_element_type=jnp.float32,
    )
    down_share = lax.psum_scatter(
        down_terms.astype(jnp.bfloat16), "tensor", scatter_dimension=1, tiled=True
    ).astype(jnp.float32)
    return (residual.astype(jnp.float32) + down_share).astype(jnp.bfloat16)


def solution(mesh):
    return jax.shard_map(
        shards,
        mesh=mesh,
        in_specs=(
            P("seq", "tensor"),
            P(),
            P(None, None, "tensor"),
            P(None, "tensor"),
            P("tensor"),
            P(None, "tensor", None, None),
            P(None, "tensor"),
            P("tensor"),
            P("tensor", None),
            P(),
            P(None, "seq", "tensor"),
            P("tensor", "seq"),
        ),
        out_specs=P("seq", "tensor"),
        check_vma=False,
    )
```

profile of v0, /device:TPU:0, one launch (start us, length us, event | category | flops | bytes accessed | tf_op | source)
XLA Modules:
  0.0 835.9 jit_solution(12491428809460878877)
XLA Ops:
  7.4 0.7 all-gather.6.cloned.1.call-update
  8.1 0.9 fusion.115
  9.0 26.0 %all-gather.6.cloned.1.call-done = bf16[256,4096]{1,0:T(8,128)(2,1)} async-done(((bf16[256,1024]{1,0:T(8,128)(2,1)}), bf16[256,4096]{1,0:T(8,128)(2,1)}) %all-gather.6.cloned.1.call-update) | async-done | bytes 2097168 | tf_op jit(solution)/shard_map/all_gather | solution.py:54
  35.0 2.1 fusion.3
  37.2 4.1 fusion.26
  41.3 3.4 collective-permute-start
  44.7 1.3 collective-permute-done
  46.1 0.3 fusion.73
  46.5 0.3 convolution_bitcast_fusion.1
  46.8 0.6 copy.18
  47.4 0.8 reshape.41
  48.3 0.1 broadcast_add_fusion
  48.4 0.8 fusion.91
  49.2 0.3 slice.293
  49.5 0.3 slice.294
  49.8 0.3 slice.332
  50.2 0.3 slice.333
  50.6 0.1 slice.296
  50.7 0.1 slice.297
  50.8 0.1 slice.335
  50.9 0.1 slice.336
  52.0 0.2 slice.326
  52.2 0.2 slice.365
  52.4 1.4 slice.328
  53.8 1.4 slice.367
  56.2 1.7 pad.129
  58.1 2.0 add_multiply_fusion.1
  60.2 1.7 pad.128
  61.8 0.7 add_bitcast_fusion
  62.5 27.9 %all-gather.1 = f32[8,1,512]{2,1,0:T(1,128)S(1)} all-gather(f32[1,1,512]{2,1,0:T(1,128)S(1)} %add_bitcast_fusion), channel_id=1, replica_groups=mesh['seq'=8,'tensor'=4] {'seq'}, dimensions={0}, use_global_device_ids=true | all-gather | bytes 18432 | tf_op jit(solution)/shard_map/all_gather | solution.py:15
  90.4 1.6 pad.113
  92.1 1.0 pad_maximum_fusion
  93.1 1.7 pad.112
  94.7 0.7 add_bitcast_fusion.1
  95.5 26.1 %all-gather = f32[8,1,512]{2,1,0:T(1,128)S(1)} all-gather(f32[1,1,512]{2,1,0:T(1,128)S(1)} %add_bitcast_fusion.1), channel_id=1, replica_groups=mesh['seq'=8,'tensor'=4] {'seq'}, dimensions={0}, use_global_device_ids=true | all-gather | bytes 18432 | tf_op jit(solution)/shard_map/all_gather | solution.py:15
  121.6 0.4 while.14
  122.0 7.9 convolution_convert_fusion.1
  130.0 0.5 all-gather.8.cloned.1.call-update
  130.6 0.5 all-gather.10.cloned.1.call-update
  131.2 0.2 reduce-scatter.2.cloned.1.call-start
  131.4 46.4 %all-reduce.34.cloned.1.call-done = bf16[256,4096]{1,0:T(8,128)(2,1)} async-done(((bf16[256,4096]{1,0:T(8,128)(2,1)}), bf16[256,4096]{1,0:T(8,128)(2,1)}) %all-reduce.34.cloned.1.call-update) | async-done | bytes 2097168 | tf_op jit(solution)/shard_map/psum | solution.py:92
  177.8 3.9 fusion
  181.7 427.0 %all-gather.8.cloned.1.call-done = bf16[2,4096,1536]{2,1,0:T(8,128)(2,1)} async-done(((bf16[2,512,1536]{2,1,0:T(8,128)(2,1)}), bf16[2,4096,1536]{2,1,0:T(8,128)(2,1)}) %all-gather.8.cloned.1.call-update) | async-done | bytes 25165840 | tf_op jit(solution)/shard_map/all_gather | solution.py:102
  608.7 13.4 %convolution_bitcast_fusion = f32[2,256,1536]{2,1,0:T(8,128)} fusion(bf16[2,4096,1536]{2,1,0:T(8,128)(2,1)} %all-gather.8.cloned.1.call-done, bf16[256,4096]{1,0:T(8,128)(2,1)} %get-tuple-element.129, f32[4096]{0:T(1024)S(1)} %copy-done.8, f32[256]{0:T(256)S(1)} %add_rsqrt_fusion), kind=kOutput, calls=%fused_computation.23 | convolution fusion | flops 6446645248 | bytes 30426112 | tf_op jit(solution)/shard_map/tr,krf->ktf/dot_general | solution.py:99
  622.1 164.4 %all-gather.10.cloned.1.call-done = bf16[1536,4096]{1,0:T(8,128)(2,1)} async-done(((bf16[1536,512]{1,0:T(8,128)(2,1)}), bf16[1536,4096]{1,0:T(8,128)(2,1)}) %all-gather.10.cloned.1.call-update) | async-done | bytes 12582928 | tf_op jit(solution)/shard_map/all_gather | solution.py:108
  786.5 10.6 %convolution_convert_fusion = bf16[256,4096]{1,0:T(8,128)(2,1)} fusion(bf16[1536,4096]{1,0:T(8,128)(2,1)} %all-gather.10.cloned.1.call-done, f32[2,256,1536]{2,1,0:T(8,128)} %convolution_bitcast_fusion), kind=kOutput, calls=%fused_computation.8 | convolution fusion | flops 3226206208 | bytes 17825792 | tf_op jit(solution)/shard_map/dot_general | solution.py:106
  797.1 29.5 %reduce-scatter.2.cloned.1.call-done = bf16[256,1024]{1,0:T(8,128)(2,1)} async-done(((bf16[256,4096]{1,0:T(8,128)(2,1)}), bf16[256,1024]{1,0:T(8,128)(2,1)}) %reduce-scatter.2.cloned.1.call-update) | async-done | bytes 524304 | tf_op jit(solution)/shard_map/reduce_scatter | solution.py:111
  826.6 2.2 add_convert_fusion
  (152 shorter events, 2.3 us)
Async XLA Ops:
  7.4 39.1 %copy-start = (bf16[2,2,256,256]{3,2,1,0:T(8,128)(2,1)S(1)}, bf16[2,2,256,256]{3,2,1,0:T(8,128)(2,1)}, u32[]{:S(2)}) copy-start(bf16[2,2,256,256]{3,2,1,0:T(8,128)(2,1)} %param.19) | copy-start | bytes 1572868
  7.4 27.7 %all-gather.6.cloned.1.call-start = ((), (), s32[]{:S(2)}) async-start(), calls=%async_computation.1 | async-start | bytes 2621440 | tf_op jit(solution)/shard_map/all_gather | solution.py:54
  8.1 169.7 %all-reduce.34.cloned.1.call-start = ((), (), s32[]{:S(2)}) async-start(), calls=%async_computation.2 | async-start | bytes 4194304 | tf_op jit(solution)/shard_map/psum | solution.py:92
  37.1 7.6 copy-start.6
  37.1 9.0 %copy-start.4 = (f32[512]{0:T(512)S(1)}, f32[512]{0:T(512)}, u32[]{:S(2)}) copy-start(f32[512]{0:T(512)} %param.18) | copy-start | bytes 6148
  41.3 4.7 collective-permute-start
  46.4 1.8 copy-start.5
  58.1 63.9 %copy-start.2 = (bf16[256,4096]{1,0:T(8,128)(2,1)S(1)}, bf16[256,4096]{1,0:T(8,128)(2,1)}, u32[]{:S(2)}) copy-start(bf16[256,4096]{1,0:T(8,128)(2,1)} %all-gather.6.cloned.1.call-done) | copy-start | bytes 6291460
  58.1 63.9 %copy-start.7 = (f32[4096]{0:T(1024)S(1)}, f32[4096]{0:T(1024)}, u32[]{:S(2)}) copy-start(f32[4096]{0:T(1024)} %param.15) | copy-start | bytes 49156
  60.1 61.9 %copy-start.3 = (f32[256,512]{1,0:T(8,128)S(1)}, f32[256,512]{1,0:T(8,128)}, u32[]{:S(2)}) copy-start(f32[256,512]{1,0:T(8,128)} %pad.129) | copy-start | bytes 1572868
  130.0 478.7 %all-gather.8.cloned.1.call-start = ((), (), s32[]{:S(2)}) async-start(), calls=%async_computation.3 | async-start | bytes 28311552 | tf_op jit(solution)/shard_map/all_gather | solution.py:102
  130.6 656.0 %all-gather.10.cloned.1.call-start = ((), (), s32[]{:S(2)}) async-start(), calls=%async_computation.4 | async-start | bytes 14155776 | tf_op jit(solution)/shard_map/all_gather | solution.py:108
  131.2 477.6 %copy-start.8 = (f32[4096]{0:T(1024)S(1)}, f32[4096]{0:T(1024)}, u32[]{:S(2)}) copy-start(f32[4096]{0:T(1024)} %param.23) | copy-start | bytes 49156
  131.2 695.4 %reduce-scatter.2.cloned.1.call-start = ((), (), s32[]{:S(2)}) async-start(), calls=%async_computation.5 | async-start | bytes 2621440 | tf_op jit(solution)/shard_map/reduce_scatter | solution.py:111
  786.5 42.3 %copy-start.1 = (bf16[2,2,256,256]{3,2,1,0:T(8,128)(2,1)S(1)}, bf16[2,2,256,256]{3,2,1,0:T(8,128)(2,1)}, u32[]{:S(2)}) copy-start(bf16[2,2,256,256]{3,2,1,0:T(8,128)(2,1)} %param.19) | copy-start | bytes 1572868
Sparse Core Ops, SparseCore 0:
  9.7 25.2 all-gather.5
  130.1 47.6 all-reduce.33
  797.2 29.3 reduce-scatter.1
Sparse Core Ops, SparseCore 1:
  132.0 476.6 all-gather.7
  610.6 175.9 all-gather.9
where the time goes:
time: 836 us
  waiting for transfers between devices  696 us (83%)
  blocking collectives  54 us (6%)
  matrix products  36.4 us (4%)
  between operations  15.4 us (2%)
  local copies, waits for them, and re-layouts  15.1 us (2%)
  other arithmetic  14.7 us (2%)
    all_gather x1, waiting for transfers between devices, shards(): lax.all_gather(mlp_in, 'seq', axis=1, tiled=True)  427 us
    all_gather x1, waiting for transfers between devices, shards(): lax.all_gather(mlp_out, 'seq', axis=1, tiled=True)  164 us
    all_gather x2, blocking collectives, prefix(): everything = jax.tree.map(lambda part: lax.all_gather(part, axis), value)  54 us
    psum x1, waiting for transfers between devices, shards(): lax.psum(partial_sums.astype(jnp.bfloat16), 'tensor').astype(jnp.float32)  46.4 us
    reduce_scatter x1, waiting for transfers between devices, shards(): lax.psum_scatter(down_terms.astype(jnp.bfloat16), 'tensor', scatter_dimen...  29.5 us
    all_gather x1, waiting for transfers between devices, shards(): whole_rows = lax.all_gather(layer_input, 'tensor', axis=1, tiled=True)  26 us
  transfers between devices with their start and end apart: 6, of which 6 were waited for; matrix products, arithmetic and copies ran while one was open for 2% of the time, Pallas kernels for 0%

commit v1 on v0

--- a/solution.py
+++ b/solution.py
@@ -89,7 +89,9 @@
     state = cum_decay * carried + cum_state
     mixed = (state * branch_y).astype(jnp.bfloat16)
     partial_sums = jnp.dot(mixed, out_weight, preferred_element_type=jnp.float32)
-    full_sums = lax.psum(partial_sums.astype(jnp.bfloat16), "tensor").astype(jnp.float32)
+    full_sums = jnp.sum(lax.all_gather(partial_sums.astype(jnp.bfloat16), "tensor"), axis=0).astype(
+        jnp.float32
+    )
     mid_full = (whole_rows.astype(jnp.float32) + full_sums).astype(jnp.bfloat16)
     own_width = layer_input.shape[1]
     residual = lax.dynamic_slice_in_dim(

time: 836 us -> 891 us (1.066)
  waiting for transfers between devices: 696 us -> 747 us
    all_gather x0 -> x1, waiting for transfers between devices: none -> 53.2 us  [shards(): lax.all_gather(partial_sums.astype(jnp.bfloat16), 'tensor')]
    psum x1 -> x0, waiting for transfers between devices: 46.4 us -> none  [shards(): lax.psum(partial_sums.astype(jnp.bfloat16), 'tensor').astype(jnp.float32)]
    all_gather x1, waiting for transfers between devices: 427 us -> 471 us  [shards(): lax.all_gather(mlp_in, 'seq', axis=1, tiled=True)]
  transfers between devices with their start and end apart: 6 -> 6, of which waited for: 6 -> 6; matrix products, arithmetic and copies ran while one was open for 2% -> 3% of each run, Pallas kernels for 0% -> 0%
where the time goes in v1:
time: 891 us
  waiting for transfers between devices  747 us (84%)
  blocking collectives  54 us (6%)
  matrix products  36.4 us (4%)
  other arithmetic  21.7 us (2%)
  between operations  14 us (2%)
  local copies, waits for them, and re-layouts  13.5 us (2%)
    all_gather x1, waiting for transfers between devices, shards(): lax.all_gather(mlp_in, 'seq', axis=1, tiled=True)  471 us
    all_gather x1, waiting for transfers between devices, shards(): lax.all_gather(mlp_out, 'seq', axis=1, tiled=True)  165 us
    all_gather x2, blocking collectives, prefix(): everything = jax.tree.map(lambda part: lax.all_gather(part, axis), value)  54 us
    all_gather x1, waiting for transfers between devices, shards(): lax.all_gather(partial_sums.astype(jnp.bfloat16), 'tensor')  53.2 us
    reduce_scatter x1, waiting for transfers between devices, shards(): lax.psum_scatter(down_terms.astype(jnp.bfloat16), 'tensor', scatter_dimen...  29.5 us
    all_gather x1, waiting for transfers between devices, shards(): whole_rows = lax.all_gather(layer_input, 'tensor', axis=1, tiled=True)  26 us
  transfers between devices with their start and end apart: 6, of which 6 were waited for; matrix products, arithmetic and copies ran while one was open for 3% of the time, Pallas kernels for 0%

profile of v1, /device:TPU:0, one launch (start us, length us, event | category | flops | bytes accessed | tf_op | source)
XLA Modules:
  0.0 890.9 jit_solution(2056601713183165907)
XLA Ops:
  6.5 0.7 all-gather.8.cloned.1.call-update
  7.3 0.9 fusion.115
  8.2 26.0 %all-gather.8.cloned.1.call-done = bf16[256,4096]{1,0:T(8,128)(2,1)} async-done(((bf16[256,1024]{1,0:T(8,128)(2,1)}), bf16[256,4096]{1,0:T(8,128)(2,1)}) %all-gather.8.cloned.1.call-update) | async-done | bytes 2097168 | tf_op jit(solution)/shard_map/all_gather | solution.py:54
  34.2 2.1 fusion.3
  36.3 4.1 fusion.26
  40.5 3.4 collective-permute-start
  43.9 1.3 collective-permute-done
  45.3 0.3 fusion.73
  45.6 0.3 convolution_bitcast_fusion.1
  46.0 0.6 copy.18
  46.6 0.8 reshape.41
  47.4 0.1 broadcast_add_fusion
  47.6 0.8 fusion.91
  48.3 0.3 slice.293
  48.7 0.3 slice.294
  49.0 0.3 slice.332
  49.3 0.3 slice.333
  49.7 0.1 slice.296
  49.9 0.1 slice.297
  50.0 0.1 slice.335
  50.1 0.1 slice.336
  51.1 0.2 slice.326
  51.3 0.2 slice.365
  51.6 1.4 slice.328
  53.0 1.4 slice.367
  55.4 1.7 pad.129
  57.2 1.9 add_multiply_fusion.1
  59.2 0.7 add_bitcast_fusion
  59.9 27.9 %all-gather.2 = f32[8,1,512]{2,1,0:T(1,128)S(1)} all-gather(f32[1,1,512]{2,1,0:T(1,128)S(1)} %add_bitcast_fusion), channel_id=1, replica_groups=mesh['seq'=8,'tensor'=4] {'seq'}, dimensions={0}, use_global_device_ids=true | all-gather | bytes 18432 | tf_op jit(solution)/shard_map/all_gather | solution.py:15
  87.8 1.7 pad.113
  89.5 1.0 pad_maximum_fusion
  90.5 1.7 pad.112
  92.1 0.7 add_bitcast_fusion.1
  92.9 26.1 %all-gather.1 = f32[8,1,512]{2,1,0:T(1,128)S(1)} all-gather(f32[1,1,512]{2,1,0:T(1,128)S(1)} %add_bitcast_fusion.1), channel_id=1, replica_groups=mesh['seq'=8,'tensor'=4] {'seq'}, dimensions={0}, use_global_device_ids=true | all-gather | bytes 18432 | tf_op jit(solution)/shard_map/all_gather | solution.py:15
  119.0 0.4 while.14
  119.4 7.9 convolution_convert_fusion.1
  127.4 0.7 all-gather.10.cloned.1.call-update
  128.2 0.5 all-gather.12.cloned.1.call-update
  128.7 0.2 reduce-scatter.2.cloned.1.call-start
  128.9 53.2 %all-gather.14.cloned.1.call-done = bf16[1024,4096]{1,0:T(8,128)(2,1)} async-done(((bf16[256,4096]{1,0:T(8,128)(2,1)}), bf16[1024,4096]{1,0:T(8,128)(2,1)}) %all-gather.14.cloned.1.call-update) | async-done | bytes 8388624 | tf_op jit(solution)/shard_map/all_gather | solution.py:92
  182.1 6.9 reduce_sum.31
  189.0 4.1 fusion
  193.2 470.9 %all-gather.10.cloned.1.call-done = bf16[2,4096,1536]{2,1,0:T(8,128)(2,1)} async-done(((bf16[2,512,1536]{2,1,0:T(8,128)(2,1)}), bf16[2,4096,1536]{2,1,0:T(8,128)(2,1)}) %all-gather.10.cloned.1.call-update) | async-done | bytes 25165840 | tf_op jit(solution)/shard_map/all_gather | solution.py:104
  664.1 13.4 %convolution_bitcast_fusion = f32[2,256,1536]{2,1,0:T(8,128)} fusion(bf16[2,4096,1536]{2,1,0:T(8,128)(2,1)} %all-gather.10.cloned.1.call-done, bf16[256,4096]{1,0:T(8,128)(2,1)} %get-tuple-element.129, f32[4096]{0:T(1024)S(1)} %copy-done.7, f32[256]{0:T(256)S(1)} %add_rsqrt_fusion), kind=kOutput, calls=%fused_computation.23 | convolution fusion | flops 6446645248 | bytes 30426112 | tf_op jit(solution)/shard_map/tr,krf->ktf/dot_general | solution.py:101
  677.5 164.6 %all-gather.12.cloned.1.call-done = bf16[1536,4096]{1,0:T(8,128)(2,1)} async-done(((bf16[1536,512]{1,0:T(8,128)(2,1)}), bf16[1536,4096]{1,0:T(8,128)(2,1)}) %all-gather.12.cloned.1.call-update) | async-done | bytes 12582928 | tf_op jit(solution)/shard_map/all_gather | solution.py:110
  842.1 10.6 %convolution_convert_fusion = bf16[256,4096]{1,0:T(8,128)(2,1)} fusion(bf16[1536,4096]{1,0:T(8,128)(2,1)} %all-gather.12.cloned.1.call-done, f32[2,256,1536]{2,1,0:T(8,128)} %convolution_bitcast_fusion), kind=kOutput, calls=%fused_computation.8 | convolution fusion | flops 3226206208 | bytes 17825792 | tf_op jit(solution)/shard_map/dot_general | solution.py:108
  852.7 29.5 %reduce-scatter.2.cloned.1.call-done = bf16[256,1024]{1,0:T(8,128)(2,1)} async-done(((bf16[256,4096]{1,0:T(8,128)(2,1)}), bf16[256,1024]{1,0:T(8,128)(2,1)}) %reduce-scatter.2.cloned.1.call-update) | async-done | bytes 524304 | tf_op jit(solution)/shard_map/reduce_scatter | solution.py:113
  882.2 2.2 add_convert_fusion
  (151 shorter events, 2.4 us)
Async XLA Ops:
  6.5 39.1 %copy-start = (bf16[2,2,256,256]{3,2,1,0:T(8,128)(2,1)S(1)}, bf16[2,2,256,256]{3,2,1,0:T(8,128)(2,1)}, u32[]{:S(2)}) copy-start(bf16[2,2,256,256]{3,2,1,0:T(8,128)(2,1)} %param.19) | copy-start | bytes 1572868
  6.5 27.7 %all-gather.8.cloned.1.call-start = ((), (), s32[]{:S(2)}) async-start(), calls=%async_computation.1 | async-start | bytes 2621440 | tf_op jit(solution)/shard_map/all_gather | solution.py:54
  7.3 174.9 %all-gather.14.cloned.1.call-start = ((), (), s32[]{:S(2)}) async-start(), calls=%async_computation.5 | async-start | bytes 10485760 | tf_op jit(solution)/shard_map/all_gather | solution.py:92
  36.3 7.6 copy-start.5
  36.3 9.0 %copy-start.3 = (f32[512]{0:T(512)S(1)}, f32[512]{0:T(512)}, u32[]{:S(2)}) copy-start(f32[512]{0:T(512)} %param.18) | copy-start | bytes 6148
  40.5 4.7 collective-permute-start
  45.3 2.1 copy-start.4
  55.4 64.0 %copy-start.2 = (bf16[256,4096]{1,0:T(8,128)(2,1)S(1)}, bf16[256,4096]{1,0:T(8,128)(2,1)}, u32[]{:S(2)}) copy-start(bf16[256,4096]{1,0:T(8,128)(2,1)} %all-gather.8.cloned.1.call-done) | copy-start | bytes 6291460
  55.4 64.0 %copy-start.6 = (f32[4096]{0:T(1024)S(1)}, f32[4096]{0:T(1024)}, u32[]{:S(2)}) copy-start(f32[4096]{0:T(1024)} %param.15) | copy-start | bytes 49156
  127.4 536.7 %all-gather.10.cloned.1.call-start = ((), (), s32[]{:S(2)}) async-start(), calls=%async_computation.2 | async-start | bytes 28311552 | tf_op jit(solution)/shard_map/all_gather | solution.py:104
  128.1 714.0 %all-gather.12.cloned.1.call-start = ((), (), s32[]{:S(2)}) async-start(), calls=%async_computation.3 | async-start | bytes 14155776 | tf_op jit(solution)/shard_map/all_gather | solution.py:110
  128.7 753.5 %reduce-scatter.2.cloned.1.call-start = ((), (), s32[]{:S(2)}) async-start(), calls=%async_computation.4 | async-start | bytes 2621440 | tf_op jit(solution)/shard_map/reduce_scatter | solution.py:113
  189.0 475.0 %copy-start.7 = (f32[4096]{0:T(1024)S(1)}, f32[4096]{0:T(1024)}, u32[]{:S(2)}) copy-start(f32[4096]{0:T(1024)} %param.23) | copy-start | bytes 49156
  842.1 42.3 %copy-start.1 = (bf16[2,2,256,256]{3,2,1,0:T(8,128)(2,1)S(1)}, bf16[2,2,256,256]{3,2,1,0:T(8,128)(2,1)}, u32[]{:S(2)}) copy-start(bf16[2,2,256,256]{3,2,1,0:T(8,128)(2,1)} %param.19) | copy-start | bytes 1572868
Sparse Core Ops, SparseCore 0:
  8.9 25.2 all-gather.7
  127.5 54.5 all-gather.13
  183.7 480.3 all-gather.9
  666.0 176.0 all-gather.11
  852.8 29.3 reduce-scatter.1
